TPU v7x, 512 devices: a whole 4x4x16 slice. The times are simulated.
512 devices in a mesh: gx: 16 (over y, x), gy: 32 (over z, core).
Axes of the slice: x: 4, y: 4, z: 16, core: 2. Of those that a mesh axis runs over, the one named last changes fastest.
Arguments:
- posterior: bfloat16 [131072, 1000], P(('gx', 'gy')), may hold values from -6 to 6
- class_affinity: bfloat16 [131072, 1000], P(('gx', 'gy')), may hold values from 0.049804688 to 20
- band_tiles: bfloat16 [1024, 4, 128, 128], P(('gx', 'gy')), may hold values from 9.9658966e-05 to 1
- band_offset: int32 [1024, 4], P(('gx', 'gy')), may hold values from -1 to 1
- band_count: int32 [1024], P(('gx', 'gy')), may hold values from 1 to 4
- far_tiles: bfloat16 [512, 16, 128, 128], P(('gx', 'gy')), may hold values from 9.9658966e-05 to 1
- far_row: int32 [512, 16], P(('gx', 'gy')), may hold values from 0 to 1
- far_block: int32 [512, 16], P(('gx', 'gy')), may hold values from 0 to 1
Outputs:
- propagated: bfloat16 [131072, 1000], P(('gx', 'gy'))
Inputs may be any that keep to these rules, and one draw needn't show every extreme that they name: Near tiles of a slot index at or above band_count of their row block are not part of the graph.
All inputs are finite; a program needn't handle non-finite values.
Results may differ from a plain program's by a relative error of at most 0.002.
Values may be sent and summed in bfloat16 or wider, within the bound.
No kernel may reach another device: no remote copies, remote signals or barrier semaphores. Data moves between devices by JAX's collectives and lax.ppermute only.
A program may use at most 64 MiB of HBM per device.

v0:
```python
import jax
import jax.numpy as jnp
from jax import lax
from jax.sharding import PartitionSpec as P

BAND_REACH = 1
SWEEPS = 2


propagation_weight = 0.9
epsilon = 1e-06


def padded(value, sides, width):
    for axis, dim in sides:
        peers, length = (lax.axis_size(axis), value.shape[dim])
        up = [(i, (i + 1) % peers) for i in range(peers)]
        down = [(j, i) for i, j in up]
        last = lax.slice_in_dim(value, length - width, length, axis=dim)
        initial = lax.slice_in_dim(value, 0, width, axis=dim)
        before = lax.ppermute(last, axis, up)
        after = lax.ppermute(initial, axis, down)
        value = jnp.concatenate([before, value, after], axis=dim)
    return value


def normalize(mixed_rows):
    row_scale = lax.rsqrt(jnp.mean(mixed_rows * mixed_rows, axis=-1, keepdims=True) + epsilon)
    return (mixed_rows * row_scale).astype(jnp.bfloat16)


def local(
    posterior, class_affinity, band_tiles, band_offset, band_count, far_tiles, far_row, far_block
):
    row_count, class_count = posterior.shape
    tile_size = band_tiles.shape[-1]
    block_count = row_count // tile_size
    slot_count = band_tiles.shape[1]
    peer_count = lax.axis_size("gx")
    wanted = lax.all_to_all(
        far_block.reshape(peer_count), "gx", split_axis=0, concat_axis=0, tiled=True
    )
    slot_ids = jnp.arange(slot_count, dtype=jnp.int32)
    block_ids = jnp.arange(block_count, dtype=jnp.int32)
    is_live = slot_ids[None, :] < band_count[:, None]
    owner_table = (far_row.reshape(peer_count)[None, :] == block_ids[:, None]).astype(jnp.bfloat16)
    far_weights = far_tiles.reshape(peer_count, tile_size, tile_size)
    far_matrix = (
        owner_table[:, None, :, None] * jnp.transpose(far_weights, (1, 0, 2))[None]
    ).reshape(row_count, peer_count * tile_size)
    rim_depth = BAND_REACH
    source_index = block_ids[:, None] + rim_depth + band_offset
    masked_tiles = band_tiles * is_live.astype(jnp.bfloat16)[:, :, None, None]
    current = posterior
    for sweep in range(SWEEPS):
        extended = padded(current, (("gy", 0),), rim_depth * tile_size)
        outgoing = current.reshape(block_count, tile_size, class_count)[wanted].reshape(
            peer_count * tile_size, class_count
        )
        arrived = lax.all_to_all(outgoing, "gx", split_axis=0, concat_axis=0, tiled=True)
        ext_blocks = extended.reshape(-1, tile_size, class_count)
        gathered = ext_blocks[source_index]
        band_sum = jnp.einsum(
            "bsij,bsjc->bic", masked_tiles, gathered, preferred_element_type=jnp.float32
        ).reshape(row_count, class_count)
        far_sum = jnp.dot(far_matrix, arrived, preferred_element_type=jnp.float32)
        mixed_rows = propagation_weight * (band_sum + far_sum) + class_affinity.astype(jnp.float32)
        current = normalize(mixed_rows)
    return current


def solution(mesh):
    in_specs = (
        P(("gx", "gy"), None),
        P(("gx", "gy"), None),
        P(("gx", "gy"), None, None, None),
        P(("gx", "gy"), None),
        P(("gx", "gy")),
        P(("gx", "gy"), None, None, None),
        P(("gx", "gy"), None),
        P(("gx", "gy"), None),
    )
    out_specs = P(("gx", "gy"), None)
    return jax.shard_map(local, mesh=mesh, in_specs=in_specs, out_specs=out_specs, check_vma=False)
```

profile of v0, /device:TPU:480, one launch (start us, length us, event | category | flops | bytes accessed | tf_op | source)
XLA Modules:
  0.0 168.4 jit_solution(2424716360395849353)
XLA Ops:
  0.0 1.3 copy.49
  1.3 7.0 %all-to-all-start = ((s32[16,1,1]{2,1,0:T(1,128)}), s32[16,1,1]{2,1,0:T(1,128)S(1)}, u32[]{:S(2)}, u32[]{:S(2)}) async-start(s32[16,1,1]{2,1,0:T(1,128)} %copy.49), calls=%async_computation | async-start | bytes 16384 | tf_op jit(solution)/shard_map/all_to_all | solution.py:40
  8.4 1.2 copy.48
  9.6 0.3 copy.50
  9.9 6.0 %all-to-all-done = s32[16,1,1]{2,1,0:T(1,128)S(1)} async-done(((s32[16,1,1]{2,1,0:T(1,128)}), s32[16,1,1]{2,1,0:T(1,128)S(1)}, u32[]{:S(2)}, u32[]{:S(2)}) %all-to-all-start) | async-done | bytes 96 | tf_op jit(solution)/shard_map/all_to_all | solution.py:40
  15.9 0.4 reduce
  16.3 3.0 %gather_fusion.1 = bf16[16,128,1000]{1,2,0:T(8,128)(2,1)} fusion(bf16[2,128,1000]{1,2,0:T(8,128)(2,1)S(1)} %copy.50, s32[1024]{0:T(1024)S(1)} %pad_clamp_fusion), kind=kCustom, calls=%fused_computation.1 | custom fusion | bytes 8192064 | tf_op jit(solution)/shard_map/gather | solution.py:57
  19.3 0.0 copy-start.9
  19.3 4.7 %all-to-all-start.1 = ((bf16[16,128,1000]{1,2,0:T(8,128)(2,1)}), bf16[16,128,1000]{1,2,0:T(8,128)(2,1)}, u32[]{:S(2)}, u32[]{:S(2)}) async-start(bf16[16,128,1000]{1,2,0:T(8,128)(2,1)} %gather_fusion.1), calls=%async_computation.1 | async-start | bytes 8192000 | tf_op jit(solution)/shard_map/all_to_all | solution.py:60
  24.0 0.0 collective-permute-start
  24.1 1.7 %collective-permute-start.1 = (bf16[128,1000]{0,1:T(8,128)(2,1)S(1)}, bf16[128,1000]{0,1:T(8,128)(2,1)S(1)}, u32[]{:S(2)}, u32[]{:S(2)}) collective-permute-start(bf16[128,1000]{0,1:T(8,128)(2,1)S(1)} %get-tuple-element.8), channel_id=1, source_target_pairs={{1,0},{2,1},{3,2},{4,3},{5,4},{6,5},{7,6},{8,7},{9,8},{10,9},{11,1... | collective-permute-start | bytes 768008 | tf_op jit(solution)/shard_map/ppermute | solution.py:22
  25.8 0.1 compare_select_fusion
  25.9 0.1 reshape.151
  26.0 0.3 copy.47
  26.3 0.1 compare_convert_fusion.1
  26.4 0.0 copy-done.9
  26.4 1.2 broadcast_multiply_fusion
  27.6 2.2 %collective-permute-done = bf16[128,1000]{0,1:T(8,128)(2,1)S(1)} collective-permute-done((bf16[128,1000]{0,1:T(8,128)(2,1)S(1)}, bf16[128,1000]{0,1:T(8,128)(2,1)S(1)}, u32[]{:S(2)}, u32[]{:S(2)}) %collective-permute-start) | collective-permute-done | bytes 256032 | tf_op jit(solution)/shard_map/ppermute | solution.py:21
  29.8 0.0 collective-permute-done.1
  29.8 0.1 pad_maximum_fusion
  29.9 0.5 copy.44
  30.4 0.6 copy.45
  31.1 0.0 copy-start.1
  31.1 0.9 gather_fusion
  32.1 0.8 fusion.9
  32.9 1.3 copy.52
  34.1 48.6 %all-to-all-done.1 = bf16[16,128,1000]{1,2,0:T(8,128)(2,1)} async-done(((bf16[16,128,1000]{1,2,0:T(8,128)(2,1)}), bf16[16,128,1000]{1,2,0:T(8,128)(2,1)}, u32[]{:S(2)}, u32[]{:S(2)}) %all-to-all-start.1) | async-done | bytes 4096032 | tf_op jit(solution)/shard_map/all_to_all | solution.py:60
  82.8 6.4 %copy.51 = bf16[16,128,1000]{2,1,0:T(8,128)(2,1)} copy(bf16[16,128,1000]{1,2,0:T(8,128)(2,1)} %all-to-all-done.1) | data formatting | bytes 8192000 | tf_op jit(solution)/shard_map/all_to_all | solution.py:60
  89.1 0.0 copy-done.6
  89.2 4.3 %multiply_reduce_fusion.1 = (f32[256]{0:T(256)S(1)}, f32[256,1000]{0,1:T(8,128)S(1)}) fusion(bf16[256,1000]{0,1:T(8,128)(2,1)S(1)} %copy-done.6, f32[256,1000]{0,1:T(8,128)} %copy.52, bf16[2048,1000]{1,0:T(8,128)(2,1)} %bitcast.52, bf16[32,8,16,128]{3,2,1,0:T(8,128)(2,1)S(1)} %bitcast.56), kind=kOutput, calls=%fused_computation.19 | convolution fusion | flops 1050111744 | bytes 7705600 | tf_op jit(solution)/shard_map/dot_general | solution.py:66
  93.5 0.1 copy_bitcast_fusion.1
  93.6 3.0 %gather_fusion.3 = bf16[16,128,1000]{1,2,0:T(8,128)(2,1)} fusion(bf16[2,128,1000]{1,2,0:T(8,128)(2,1)S(1)} %copy_bitcast_fusion.1, s32[1024]{0:T(1024)S(1)} %pad_clamp_fusion), kind=kCustom, calls=%fused_computation.3 | custom fusion | bytes 8192064 | tf_op jit(solution)/shard_map/gather | solution.py:57
  96.6 4.5 %all-to-all-start.2 = ((bf16[16,128,1000]{1,2,0:T(8,128)(2,1)}), bf16[16,128,1000]{1,2,0:T(8,128)(2,1)}, u32[]{:S(2)}, u32[]{:S(2)}) async-start(bf16[16,128,1000]{1,2,0:T(8,128)(2,1)} %gather_fusion.3), calls=%async_computation.2 | async-start | bytes 8192000 | tf_op jit(solution)/shard_map/all_to_all | solution.py:60
  101.1 0.1 multiply_convert_fusion.1
  101.3 0.0 collective-permute-start.2
  101.3 1.7 %collective-permute-start.3 = (bf16[128,1000]{0,1:T(8,128)(2,1)S(1)}, bf16[128,1000]{0,1:T(8,128)(2,1)S(1)}, u32[]{:S(2)}, u32[]{:S(2)}) collective-permute-start(bf16[128,1000]{0,1:T(8,128)(2,1)S(1)} %get-tuple-element.6), channel_id=1, source_target_pairs={{1,0},{2,1},{3,2},{4,3},{5,4},{6,5},{7,6},{8,7},{9,8},{10,9},{11,1... | collective-permute-start | bytes 768008 | tf_op jit(solution)/shard_map/ppermute | solution.py:22
  103.0 4.0 %collective-permute-done.2 = bf16[128,1000]{0,1:T(8,128)(2,1)S(1)} collective-permute-done((bf16[128,1000]{0,1:T(8,128)(2,1)S(1)}, bf16[128,1000]{0,1:T(8,128)(2,1)S(1)}, u32[]{:S(2)}, u32[]{:S(2)}) %collective-permute-start.2) | collective-permute-done | bytes 256032 | tf_op jit(solution)/shard_map/ppermute | solution.py:21
  107.0 0.0 collective-permute-done.3
  107.0 0.1 copy_bitcast_fusion
  107.1 0.9 gather_fusion.2
  108.1 0.8 convolution_bitcast_fusion
  108.9 0.0 copy-start.3
  108.9 0.0 copy-start.7
  108.9 48.3 %all-to-all-done.2 = bf16[16,128,1000]{1,2,0:T(8,128)(2,1)} async-done(((bf16[16,128,1000]{1,2,0:T(8,128)(2,1)}), bf16[16,128,1000]{1,2,0:T(8,128)(2,1)}, u32[]{:S(2)}, u32[]{:S(2)}) %all-to-all-start.2) | async-done | bytes 4096032 | tf_op jit(solution)/shard_map/all_to_all | solution.py:60
  157.2 6.4 %copy.56 = bf16[16,128,1000]{2,1,0:T(8,128)(2,1)} copy(bf16[16,128,1000]{1,2,0:T(8,128)(2,1)} %all-to-all-done.2) | data formatting | bytes 8192000 | tf_op jit(solution)/shard_map/all_to_all | solution.py:60
  163.6 0.0 copy-done.3
  163.6 4.0 %multiply_reduce_fusion = (f32[256]{0:T(256)S(1)}, f32[256,1000]{0,1:T(8,128)S(1)}) fusion(bf16[256,1000]{0,1:T(8,128)(2,1)S(1)} %copy-done.7, bf16[2048,1000]{1,0:T(8,128)(2,1)} %bitcast.51, bf16[32,8,16,128]{3,2,1,0:T(8,128)(2,1)S(1)} %bitcast.57, f32[2,125,8,128]{3,2,1,0:T(8,128)S(1)} %convolution_bitcast_fusion), kind=kOutput, calls=%fused_computation.17 | convolution fusion | flops 1050111744 | bytes 7705600 | tf_op jit(solution)/shard_map/dot_general | solution.py:66
  167.6 0.9 multiply_convert_fusion
  (22 shorter events, 0.1 us)
Async XLA Ops:
  1.3 14.6 %all-to-all-start = ((s32[16,1,1]{2,1,0:T(1,128)}), s32[16,1,1]{2,1,0:T(1,128)S(1)}, u32[]{:S(2)}, u32[]{:S(2)}) async-start(s32[16,1,1]{2,1,0:T(1,128)} %copy.49), calls=%async_computation | async-start | bytes 16384 | tf_op jit(solution)/shard_map/all_to_all | solution.py:40
  19.3 4.7 %copy-start = (bf16[256,1000]{0,1:T(8,128)(2,1)S(1)}, bf16[256,1000]{0,1:T(8,128)(2,1)}, u32[]{:S(2)}) copy-start(bf16[256,1000]{0,1:T(8,128)(2,1)} %param.8) | copy-start | bytes 1536004
  19.3 6.5 %copy-start.5 = (s32[2,4]{1,0:T(2,128)S(1)}, s32[2,4]{1,0:T(2,128)}, u32[]{:S(2)}) copy-start(s32[2,4]{1,0:T(2,128)} %param.11) | copy-start | bytes 100
  19.3 6.7 %copy-start.4 = (bf16[1,16,128,128]{3,2,1,0:T(8,128)(2,1)S(1)}, bf16[1,16,128,128]{3,2,1,0:T(8,128)(2,1)}, u32[]{:S(2)}) copy-start(bf16[1,16,128,128]{3,2,1,0:T(8,128)(2,1)} %param.13) | copy-start | bytes 1572868
  19.3 7.0 %copy-start.8 = (s32[2]{0:T(128)S(1)}, s32[2]{0:T(128)}, u32[]{:S(2)}) copy-start(s32[2]{0:T(128)} %param.12) | copy-start | bytes 28
  19.3 7.1 %copy-start.9 = (s32[1,16]{1,0:T(1,128)S(1)}, s32[1,16]{1,0:T(1,128)}, u32[]{:S(2)}) copy-start(s32[1,16]{1,0:T(1,128)} %param.14) | copy-start | bytes 196
  19.3 63.5 %all-to-all-start.1 = ((bf16[16,128,1000]{1,2,0:T(8,128)(2,1)}), bf16[16,128,1000]{1,2,0:T(8,128)(2,1)}, u32[]{:S(2)}, u32[]{:S(2)}) async-start(bf16[16,128,1000]{1,2,0:T(8,128)(2,1)} %gather_fusion.1), calls=%async_computation.1 | async-start | bytes 8192000 | tf_op jit(solution)/shard_map/all_to_all | solution.py:60
  24.0 5.7 %collective-permute-start = (bf16[128,1000]{0,1:T(8,128)(2,1)S(1)}, bf16[128,1000]{0,1:T(8,128)(2,1)S(1)}, u32[]{:S(2)}, u32[]{:S(2)}) collective-permute-start(bf16[128,1000]{0,1:T(8,128)(2,1)S(1)} %get-tuple-element.7), channel_id=1, source_target_pairs={{0,1},{1,2},{2,3},{3,4},{4,5},{5,6},{6,7},{7,8},{8,9},{9,10},{10,1... | collective-permute-start | bytes 768008 | tf_op jit(solution)/shard_map/ppermute | solution.py:21
  24.1 5.7 %collective-permute-start.1 = (bf16[128,1000]{0,1:T(8,128)(2,1)S(1)}, bf16[128,1000]{0,1:T(8,128)(2,1)S(1)}, u32[]{:S(2)}, u32[]{:S(2)}) collective-permute-start(bf16[128,1000]{0,1:T(8,128)(2,1)S(1)} %get-tuple-element.8), channel_id=1, source_target_pairs={{1,0},{2,1},{3,2},{4,3},{5,4},{6,5},{7,6},{8,7},{9,8},{10,9},{11,1... | collective-permute-start | bytes 768008 | tf_op jit(solution)/shard_map/ppermute | solution.py:22
  31.1 1.0 copy-start.1
  34.1 55.0 %copy-start.2 = (bf16[2,128,16,128]{3,2,1,0:T(8,128)(2,1)S(1)}, bf16[2,128,16,128]{3,2,1,0:T(8,128)(2,1)}, u32[]{:S(2)}) copy-start(bf16[2,128,16,128]{3,2,1,0:T(8,128)(2,1)} %broadcast_multiply_fusion) | copy-start | bytes 3145732
  34.1 55.0 %copy-start.6 = (bf16[256,1000]{0,1:T(8,128)(2,1)S(1)}, bf16[256,1000]{0,1:T(8,128)(2,1)}, u32[]{:S(2)}) copy-start(bf16[256,1000]{0,1:T(8,128)(2,1)} %param.9) | copy-start | bytes 1536004
  96.6 60.6 %all-to-all-start.2 = ((bf16[16,128,1000]{1,2,0:T(8,128)(2,1)}), bf16[16,128,1000]{1,2,0:T(8,128)(2,1)}, u32[]{:S(2)}, u32[]{:S(2)}) async-start(bf16[16,128,1000]{1,2,0:T(8,128)(2,1)} %gather_fusion.3), calls=%async_computation.2 | async-start | bytes 8192000 | tf_op jit(solution)/shard_map/all_to_all | solution.py:60
  101.3 5.7 %collective-permute-start.2 = (bf16[128,1000]{0,1:T(8,128)(2,1)S(1)}, bf16[128,1000]{0,1:T(8,128)(2,1)S(1)}, u32[]{:S(2)}, u32[]{:S(2)}) collective-permute-start(bf16[128,1000]{0,1:T(8,128)(2,1)S(1)} %get-tuple-element.5), channel_id=1, source_target_pairs={{0,1},{1,2},{2,3},{3,4},{4,5},{5,6},{6,7},{7,8},{8,9},{9,10},{10,1... | collective-permute-start | bytes 768008 | tf_op jit(solution)/shard_map/ppermute | solution.py:21
  101.3 5.7 %collective-permute-start.3 = (bf16[128,1000]{0,1:T(8,128)(2,1)S(1)}, bf16[128,1000]{0,1:T(8,128)(2,1)S(1)}, u32[]{:S(2)}, u32[]{:S(2)}) collective-permute-start(bf16[128,1000]{0,1:T(8,128)(2,1)S(1)} %get-tuple-element.6), channel_id=1, source_target_pairs={{1,0},{2,1},{3,2},{4,3},{5,4},{6,5},{7,6},{8,7},{9,8},{10,9},{11,1... | collective-permute-start | bytes 768008 | tf_op jit(solution)/shard_map/ppermute | solution.py:22
  108.9 54.7 %copy-start.3 = (bf16[2,128,16,128]{3,2,1,0:T(8,128)(2,1)S(1)}, bf16[2,128,16,128]{3,2,1,0:T(8,128)(2,1)}, u32[]{:S(2)}) copy-start(bf16[2,128,16,128]{3,2,1,0:T(8,128)(2,1)} %broadcast_multiply_fusion) | copy-start | bytes 3145732
  108.9 54.7 %copy-start.7 = (bf16[256,1000]{0,1:T(8,128)(2,1)S(1)}, bf16[256,1000]{0,1:T(8,128)(2,1)}, u32[]{:S(2)}) copy-start(bf16[256,1000]{0,1:T(8,128)(2,1)} %param.9) | copy-start | bytes 1536004
where the time goes:
time: 169 us; the launch traced here: 168 us
  waiting for transfers between devices  109 us (64%)
  local copies, waits for them, and re-layouts  26.5 us (16%)
  starting transfers between devices  19.7 us (12%)
  matrix products  9.84 us (6%)
  other arithmetic  3.07 us (2%)
    all_to_all x2, waiting for transfers between devices, local(): lax.all_to_all(outgoing, 'gx', split_axis=0, concat_axis=0, tiled=True)  96.9 us
    all_to_all x2, local copies, waits for them, and re-layouts, local(): lax.all_to_all(outgoing, 'gx', split_axis=0, concat_axis=0, tiled=True)  12.8 us
    all_to_all x2, starting transfers between devices, local(): lax.all_to_all(outgoing, 'gx', split_axis=0, concat_axis=0, tiled=True)  9.21 us
    dot_general x2, matrix products, local(): far_sum = jnp.dot(far_matrix, arrived, preferred_element_type=jnp.float32)  8.31 us
    all_to_all x1, starting transfers between devices, local(): lax.all_to_all(far_block.reshape(peer_count), 'gx', split_axis=0, concat_...  7.03 us
    ppermute x2, waiting for transfers between devices, padded(): before = lax.ppermute(last, axis, up)  6.14 us
    gather x2, local copies, waits for them, and re-layouts, local(): current.reshape(block_count, tile_size, class_count)[wanted]  5.99 us
    all_to_all x1, waiting for transfers between devices, local(): lax.all_to_all(far_block.reshape(peer_count), 'gx', split_axis=0, concat_...  5.99 us
  transfers between devices with their start and end apart: 7, of which 5 were waited for; matrix products, arithmetic and copies ran while one was open for 6% of the time, Pallas kernels for 0%

commit v1 on v0

v1 whole, which is shorter than its diff:
```python
import jax
import jax.numpy as jnp
import numpy as np
from jax import lax
from jax.experimental import pallas as pl
from jax.experimental.pallas import tpu as pltpu
from jax.sharding import Mesh, PartitionSpec as P

SWEEPS = 2
SIDE = 4
PEERS = 4
CODE_ROWS = 16
CODE_BITS = 13
CHUNK = 112
POWER_ROWS = 8

propagation_weight = 0.9
epsilon = 1e-06

VMEM = pl.BlockSpec(memory_space=pltpu.VMEM)
SMEM = pl.BlockSpec(memory_space=pltpu.SMEM)
MIB = 1024 * 1024


def squares(shift):
    return [
        [((2 * i + k - shift) % SIDE) * SIDE + (2 * j + m - shift) % SIDE for k in (0, 1) for m in (0, 1)]
        for i in (0, 1)
        for j in (0, 1)
    ]


def phase_squares(core, phase):
    return squares((core + phase) % 2)


def phase_groups(inner, phase):
    return [
        [chip * inner + pos for chip in square]
        for pos in range(inner)
        for square in phase_squares(pos % 2, phase)
    ]


def tile_order():
    order = np.zeros((2, SIDE * SIDE, PEERS, PEERS), np.int32)
    for core in range(2):
        first = {chip: square for square in phase_squares(core, 0) for chip in square}
        second = {chip: square for square in phase_squares(core, 1) for chip in square}
        for chip in range(SIDE * SIDE):
            for b, middle in enumerate(second[chip]):
                order[core, chip, b] = first[middle]
    return order


def pack_kernel(order_ref, row_ref, block_ref, tiles_ref, out_ref):
    size = tiles_ref.shape[-1]
    blocks = 2
    for b in range(PEERS):
        sublane = lax.broadcasted_iota(jnp.int32, (CODE_ROWS, size), 0)
        codes = jnp.zeros((CODE_ROWS, size), jnp.float32)
        for a in range(PEERS):
            q = order_ref[b, a]
            out_ref[b, a * size : (a + 1) * size, :] = tiles_ref[q]
            code = (row_ref[q] * blocks + block_ref[q]).astype(jnp.float32)
            codes = jnp.where(sublane == a, code, codes)
        out_ref[b, PEERS * size :, :] = codes.astype(jnp.bfloat16)


def pack(order, row, block, tiles):
    size = tiles.shape[-1]
    return pl.pallas_call(
        pack_kernel,
        out_shape=jax.ShapeDtypeStruct((PEERS, PEERS * size + CODE_ROWS, size), jnp.bfloat16),
        in_specs=[SMEM, SMEM, SMEM, VMEM],
        out_specs=VMEM,
        compiler_params=pltpu.CompilerParams(vmem_limit_bytes=4 * MIB),
        name="pack",
    )(order, row, block, tiles)


def times_transposed(left, right):
    return lax.dot_general(left, right, (((1,), (1,)), ((), ())), preferred_element_type=jnp.float32)


def near_kernel(offset_ref, count_ref, before_ref, own_ref, after_ref, tiles_ref, sum_ref, ext, left, right):
    blocks, slots, size, _ = tiles_ref.shape
    ext[0] = before_ref[...]
    for b in range(blocks):
        ext[b + 1] = own_ref[:, b * size : (b + 1) * size]
    ext[blocks + 1] = after_ref[...]
    for b in range(blocks):
        for s in range(slots):
            tile = tiles_ref[b, s]
            right[:, s * size : (s + 1) * size] = jnp.where(s < count_ref[b], tile, jnp.zeros_like(tile))
            left[:, s * size : (s + 1) * size] = ext[b + 1 + offset_ref[b, s]]
        sum_ref[:, b * size : (b + 1) * size] = times_transposed(left[...], right[...])


def near_sum(offset, count, before, own, after, tiles):
    blocks, slots, size, _ = tiles.shape
    classes = own.shape[0]
    return pl.pallas_call(
        near_kernel,
        out_shape=jax.ShapeDtypeStruct((classes, blocks * size), jnp.float32),
        in_specs=[SMEM, SMEM, VMEM, VMEM, VMEM, VMEM],
        out_specs=VMEM,
        scratch_shapes=[
            pltpu.VMEM((blocks + 2, classes, size), jnp.bfloat16),
            pltpu.VMEM((classes, slots * size), jnp.bfloat16),
            pltpu.VMEM((size, slots * size), jnp.bfloat16),
        ],
        cost_estimate=pl.CostEstimate(flops=3_000_000_000, bytes_accessed=3_000_000, transcendentals=0),
        compiler_params=pltpu.CompilerParams(vmem_limit_bytes=12 * MIB),
        name="near_sum",
    )(offset, count, before, own, after, tiles)


def partial_kernel(code_ref, rows_ref, tiles_ref, out_ref, left, right, acc):
    d = pl.program_id(0)
    peers, classes, width = rows_ref.shape
    size = tiles_ref.shape[-1]
    blocks = width // size
    height = out_ref.shape[1]
    for a in range(peers):
        code = code_ref[d, a]
        tile = tiles_ref[0, a * size : (a + 1) * size, :]
        for r in range(blocks):
            right[r * size : (r + 1) * size, a * size : (a + 1) * size] = jnp.where(
                code // blocks == r, tile, jnp.zeros_like(tile)
            )
        lane = pl.multiple_of((code % blocks) * size, size)
        left[:, a * size : (a + 1) * size] = rows_ref[a, :, pl.ds(lane, size)]
    acc[:classes, :] = times_transposed(left[...], right[...])
    acc[classes:, :] = jnp.zeros((height - classes, width), jnp.float32)
    peak = jnp.max(jnp.abs(acc[...]), axis=0, keepdims=True)
    power = jnp.floor(jnp.log2(jnp.maximum(peak, 1e-30)))
    scale = jnp.exp2(CODE_BITS - power)
    for at in range(0, height, CHUNK):
        scaled = jnp.round(acc[at : at + CHUNK, :] * scale)
        if at + CHUNK > classes:
            sublane = lax.broadcasted_iota(jnp.int32, scaled.shape, 0) + at
            scaled = jnp.where(sublane < classes, scaled, power)
        out_ref[0, at : at + CHUNK, :] = scaled.astype(jnp.int32).astype(jnp.int16)


def partial_sums(code, rows, tiles):
    peers, classes, width = rows.shape
    size = tiles.shape[-1]
    height = classes + POWER_ROWS
    return pl.pallas_call(
        partial_kernel,
        out_shape=jax.ShapeDtypeStruct((peers, height, width), jnp.int16),
        grid=(peers,),
        in_specs=[
            SMEM,
            pl.BlockSpec((peers, classes, width), lambda d: (0, 0, 0)),
            pl.BlockSpec((1, tiles.shape[1], size), lambda d: (d, 0, 0)),
        ],
        out_specs=pl.BlockSpec((1, height, width), lambda d: (d, 0, 0)),
        scratch_shapes=[
            pltpu.VMEM((classes, peers * size), jnp.bfloat16),
            pltpu.VMEM((width, peers * size), jnp.bfloat16),
            pltpu.VMEM((height, width), jnp.float32),
        ],
        compiler_params=pltpu.CompilerParams(vmem_limit_bytes=16 * MIB),
        name="partial_sums",
    )(code, rows, tiles)


def combine_kernel(copies, near_ref, parts_ref, affinity_ref, *refs):
    peers = parts_ref.shape[0]
    classes, width = near_ref.shape
    out_refs, mixed_ref = refs[:-1], refs[-1]
    power_at = classes - POWER_ROWS
    scales = []
    for p in range(peers):
        power = parts_ref[p, power_at:, :].astype(jnp.int32).astype(jnp.float32)[POWER_ROWS : POWER_ROWS + 1, :]
        scales.append(jnp.exp2(power - CODE_BITS))
    square = jnp.zeros((1, width), jnp.float32)
    for start in range(0, classes, CHUNK):
        at = slice(start, min(start + CHUNK, classes))
        total = near_ref[at, :]
        for p in range(peers):
            total += parts_ref[p, at, :].astype(jnp.int32).astype(jnp.float32) * scales[p]
        mixed = propagation_weight * total + affinity_ref[at, :].astype(jnp.float32)
        mixed_ref[at, :] = mixed
        square += jnp.sum(mixed * mixed, axis=0, keepdims=True)
    row_scale = lax.rsqrt(square * (1.0 / classes) + epsilon)
    for start in range(0, classes, CHUNK):
        at = slice(start, min(start + CHUNK, classes))
        result = (mixed_ref[at, :] * row_scale).astype(jnp.bfloat16)
        out_refs[0][at, :] = result
        for n in range(copies):
            out_refs[1][n, at, :] = result


def combine(near, parts, affinity, copies):
    shapes = [jax.ShapeDtypeStruct(near.shape, jnp.bfloat16)]
    if copies:
        shapes.append(jax.ShapeDtypeStruct((copies,) + near.shape, jnp.bfloat16))
    return pl.pallas_call(
        lambda *refs: combine_kernel(copies, *refs),
        out_shape=shapes,
        in_specs=[VMEM, VMEM, VMEM],
        out_specs=[VMEM] * len(shapes),
        scratch_shapes=[pltpu.VMEM(near.shape, jnp.float32)],
        compiler_params=pltpu.CompilerParams(vmem_limit_bytes=16 * MIB),
        name="combine",
    )(near, parts, affinity)


def local(inner, posterior, class_affinity, band_tiles, band_offset, band_count, far_tiles, far_row, far_block):
    size = band_tiles.shape[2]
    chips = SIDE * SIDE
    ring = [(x * inner + j, x * inner + (j + 1) % inner) for x in range(chips) for j in range(inner)]
    back = [(j, i) for i, j in ring]
    device = lax.axis_index("d")
    order = jnp.asarray(tile_order())[(device % inner) % 2, device // inner]

    def exchange(value, phase):
        return lax.all_to_all(value, "d", 0, 0, tiled=True, axis_index_groups=phase_groups(inner, phase))

    payload = exchange(
        pack(order, far_row.reshape(chips), far_block.reshape(chips), far_tiles.reshape(chips, size, size)), 1
    )
    code = payload[:, PEERS * size : PEERS * size + PEERS, 0].astype(jnp.int32)

    current = posterior.T
    affinity = class_affinity.T
    copies = jnp.broadcast_to(current[None], (PEERS,) + current.shape)
    for sweep in range(SWEEPS):
        arrived = exchange(copies, 0)
        before = lax.ppermute(current[:, -size:], "d", ring)
        after = lax.ppermute(current[:, :size], "d", back)
        near = near_sum(band_offset, band_count, before, current, after, band_tiles)
        parts = exchange(partial_sums(code, arrived, payload), 1)
        last = sweep == SWEEPS - 1
        result = combine(near, parts, affinity, 0 if last else PEERS)
        if last:
            return result[0].T
        current, copies = result


def solution(mesh):
    inner = mesh.shape["gy"]
    flat = Mesh(mesh.devices.reshape(-1), ("d",))
    spec = P("d")
    return jax.shard_map(
        lambda *args: local(inner, *args), mesh=flat, in_specs=(spec,) * 8, out_specs=spec, check_vma=False
    )
```

time: 169 us -> 115 us (0.68)
  the two profiles are of different devices: /device:TPU:480 before, /device:TPU:6 now
where the time goes in v1:
time: 115 us; the launch traced here: 114 us
  waiting for transfers between devices  37.9 us (33%)
  blocking collectives  34.2 us (30%)
  starting transfers between devices  16.5 us (14%)
  Pallas kernels  12.7 us (11%)
  local copies, waits for them, and re-layouts  12.6 us (11%)
    all_to_all x2, blocking collectives, exchange(): lax.all_to_all(value, 'd', 0, 0, tiled=True, axis_index_groups=phase_grou...  34.2 us
    all_to_all x3, waiting for transfers between devices, exchange(): lax.all_to_all(value, 'd', 0, 0, tiled=True, axis_index_groups=phase_grou...  20.7 us
    all_to_all x3, starting transfers between devices, exchange(): lax.all_to_all(value, 'd', 0, 0, tiled=True, axis_index_groups=phase_grou...  15 us
    unnamed x30, local copies, waits for them, and re-layouts  10.4 us
    ppermute x2, waiting for transfers between devices, local(): before = lax.ppermute(current[:, -size:], 'd', ring)  10.1 us
    ppermute x2, waiting for transfers between devices, local(): after = lax.ppermute(current[:, :size], 'd', back)  7.14 us
    pallas_call x2, Pallas kernels, partial_sums(): pl.pallas_call(partial_kernel, out_shape=jax.ShapeDtypeStruct((peers, hei...  6.4 us
    pallas_call x2, Pallas kernels, near_sum(): pl.pallas_call(near_kernel, out_shape=jax.ShapeDtypeStruct((classes, bloc...  3.21 us
  transfers between devices with their start and end apart: 7, of which 7 were waited for; matrix products, arithmetic and copies ran while one was open for 0% of the time, Pallas kernels for 3%

profile of v1, /device:TPU:6, one launch (start us, length us, event | category | flops | bytes accessed | tf_op | source)
XLA Modules:
  0.0 114.3 jit_solution(1240700229546624522)
XLA Ops:
  0.0 0.0 copy-start.2
  0.0 0.7 dynamic-slice_bitcast_fusion.order_ref
  0.7 0.0 copy-start.9
  0.7 1.0 copy-done.9
  1.8 0.7 copy-done.10
  2.4 0.7 copy-done.11
  3.1 0.6 pack.1
  3.7 16.9 %all_to_all.25.tiles_ref = bf16[4,528,128]{2,1,0:T(8,128)(2,1)S(1)} all-to-all(bf16[4,528,128]{2,1,0:T(8,128)(2,1)S(1)} %pack.1), channel_id=1, replica_groups={{480,384,96,0},{416,448,32,64},{224,128,352,256},{160,192,288,320},{1,3..., dimensions={0} | all-to-all | bytes 1081344 | tf_op jit(solution)/shard_map/all_to_all | solution.py:222
  20.7 0.0 copy-done.2
  20.7 1.4 %broadcast_in_dim.2 = bf16[4,1000,256]{2,1,0:T(8,128)(2,1)} broadcast(bf16[1000,256]{1,0:T(8,128)(2,1)S(1)} %bitcast.8), dimensions={1,2} | broadcast | bytes 2560000 | tf_op jit(solution)/shard_map/broadcast_in_dim | solution.py:231
  22.1 3.6 %all-to-all-start.1 = ((bf16[4,1000,256]{2,1,0:T(8,128)(2,1)}), bf16[4,1000,256]{2,1,0:T(8,128)(2,1)S(1)}, u32[]{:S(2)}, u32[]{:S(2)}) async-start(bf16[4,1000,256]{2,1,0:T(8,128)(2,1)} %broadcast_in_dim.2), calls=%async_computation.1 | async-start | bytes 4096000 | tf_op jit(solution)/shard_map/all_to_all | solution.py:222
  25.7 0.1 convert_reduce_fusion.code_ref
  25.9 13.7 %all-to-all-done.1.rows_ref = bf16[4,1000,256]{2,1,0:T(8,128)(2,1)S(1)} async-done(((bf16[4,1000,256]{2,1,0:T(8,128)(2,1)}), bf16[4,1000,256]{2,1,0:T(8,128)(2,1)S(1)}, u32[]{:S(2)}, u32[]{:S(2)}) %all-to-all-start.1) | async-done | bytes 2048032 | tf_op jit(solution)/shard_map/all_to_all | solution.py:222
  39.6 3.2 %partial_sums.2 = s16[4,1008,256]{2,1,0:T(8,128)(2,1)S(1)} custom-call(s32[4,4]{1,0:T(4,128)S(1)} %convert_reduce_fusion.code_ref, bf16[4,1000,256]{2,1,0:T(8,128)(2,1)S(1)} %all-to-all-done.1.rows_ref, bf16[4,528,128]{2,1,0:T(8,128)(2,1)S(1)} %all_to_all.25.tiles_ref), custom_call_target="tpu_custom_call" | custom-call | tf_op jit(solution)/shard_map/partial_sums/pallas_call | solution.py:151
  42.8 0.0 copy-start.1
  42.8 1.3 %copy-done.1 = s16[4,1008,256]{2,1,0:T(8,128)(2,1)} copy-done((s16[4,1008,256]{2,1,0:T(8,128)(2,1)}, s16[4,1008,256]{2,1,0:T(8,128)(2,1)S(1)}, u32[]{:S(2)}) %copy-start.1) | copy-done | bytes 2064408
  44.1 6.3 %all-to-all-start.2 = ((s16[4,1008,256]{2,1,0:T(8,128)(2,1)}), s16[4,1008,256]{2,1,0:T(8,128)(2,1)S(1)}, u32[]{:S(2)}, u32[]{:S(2)}) async-start(s16[4,1008,256]{2,1,0:T(8,128)(2,1)} %copy-done.1), calls=%async_computation.2 | async-start | bytes 4128768 | tf_op jit(solution)/shard_map/all_to_all | solution.py:222
  50.5 1.1 collective-permute-start.1
  51.5 0.0 collective-permute-start
  51.5 3.8 %collective-permute-done.1.after_ref = bf16[1000,128]{1,0:T(8,128)(2,1)S(1)} collective-permute-done((bf16[1000,128]{1,0:T(8,128)(2,1)S(1)}, bf16[1000,128]{1,0:T(8,128)(2,1)S(1)}, u32[]{:S(2)}, u32[]{:S(2)}) %collective-permute-start.1) | collective-permute-done | bytes 256032 | tf_op jit(solution)/shard_map/ppermute | solution.py:235
  55.3 4.5 %collective-permute-done.before_ref = bf16[1000,128]{1,0:T(8,128)(2,1)S(1)} collective-permute-done((bf16[1000,128]{1,0:T(8,128)(2,1)S(1)}, bf16[1000,128]{1,0:T(8,128)(2,1)S(1)}, u32[]{:S(2)}, u32[]{:S(2)}) %collective-permute-start) | collective-permute-done | bytes 256032 | tf_op jit(solution)/shard_map/ppermute | solution.py:234
  59.9 0.0 copy-done.12
  59.9 0.0 copy-done.13
  59.9 0.0 copy-done.14
  59.9 1.6 %near_sum.2.refs_0_ = f32[1000,256]{1,0:T(8,128)S(1)} custom-call(s32[2,4]{1,0:T(2,128)S(1)} %copy-done.13, s32[2]{0:T(128)S(1)} %copy-done.14, bf16[1000,128]{1,0:T(8,128)(2,1)S(1)} %collective-permute-done.before_ref, bf16[1000,256]{1,0:T(8,128)(2,1)S(1)} %bitcast.10, bf16[1000,128]{1,0:T(8,128)(2,1)S(1)} %collective-permute-done.1.after_ref, ...), custom_call_target="tpu_custom_call" | custom-call | flops 3000000000 | bytes 3000000 | tf_op jit(solution)/shard_map/near_sum/pallas_call | solution.py:103
  61.5 0.0 copy-start.5
  61.5 1.0 copy-done.5
  62.5 3.5 %all-to-all-done.2.refs_1_ = s16[4,1008,256]{2,1,0:T(8,128)(2,1)S(1)} async-done(((s16[4,1008,256]{2,1,0:T(8,128)(2,1)}), s16[4,1008,256]{2,1,0:T(8,128)(2,1)S(1)}, u32[]{:S(2)}, u32[]{:S(2)}) %all-to-all-start.2) | async-done | bytes 2064416 | tf_op jit(solution)/shard_map/all_to_all | solution.py:222
  65.9 1.0 copy-done.3
  67.0 1.2 %copy-done.6 = f32[1000,256]{1,0:T(8,128)S(1)} copy-done((f32[1000,256]{1,0:T(8,128)S(1)}, f32[1000,256]{1,0:T(8,128)}, u32[]{:S(2)}) %copy-start.6) | copy-done | bytes 1024024
  68.2 0.9 combine.2
  69.1 17.3 %all_to_all.26.rows_ref = bf16[4,1000,256]{2,1,0:T(8,128)(2,1)S(1)} all-to-all(bf16[4,1000,256]{2,1,0:T(8,128)(2,1)S(1)} %get-tuple-element.8), channel_id=1, replica_groups={{0,32,128,160},{64,96,192,224},{256,288,384,416},{320,352,448,480},{481..., dimensions={0} | all-to-all | bytes 4096000 | tf_op jit(solution)/shard_map/all_to_all | solution.py:222
  86.4 3.2 %partial_sums.3 = s16[4,1008,256]{2,1,0:T(8,128)(2,1)S(1)} custom-call(s32[4,4]{1,0:T(4,128)S(1)} %convert_reduce_fusion.code_ref, bf16[4,1000,256]{2,1,0:T(8,128)(2,1)S(1)} %all_to_all.26.rows_ref, bf16[4,528,128]{2,1,0:T(8,128)(2,1)S(1)} %all_to_all.25.tiles_ref), custom_call_target="tpu_custom_call" | custom-call | tf_op jit(solution)/shard_map/partial_sums/pallas_call | solution.py:151
  89.6 0.0 copy-start
  89.6 1.3 %copy-done = s16[4,1008,256]{2,1,0:T(8,128)(2,1)} copy-done((s16[4,1008,256]{2,1,0:T(8,128)(2,1)}, s16[4,1008,256]{2,1,0:T(8,128)(2,1)S(1)}, u32[]{:S(2)}) %copy-start) | copy-done | bytes 2064408
  90.9 5.1 %all-to-all-start.4 = ((s16[4,1008,256]{2,1,0:T(8,128)(2,1)}), s16[4,1008,256]{2,1,0:T(8,128)(2,1)S(1)}, u32[]{:S(2)}, u32[]{:S(2)}) async-start(s16[4,1008,256]{2,1,0:T(8,128)(2,1)} %copy-done), calls=%async_computation.4 | async-start | bytes 4128768 | tf_op jit(solution)/shard_map/all_to_all | solution.py:222
  96.0 0.0 collective-permute-start.3
  96.0 0.0 copy-start.4
  96.1 0.5 collective-permute-start.2
  96.5 3.3 %collective-permute-done.3.after_ref = bf16[1000,128]{1,0:T(8,128)(2,1)S(1)} collective-permute-done((bf16[1000,128]{1,0:T(8,128)(2,1)S(1)}, bf16[1000,128]{1,0:T(8,128)(2,1)S(1)}, u32[]{:S(2)}, u32[]{:S(2)}) %collective-permute-start.3) | collective-permute-done | bytes 256032 | tf_op jit(solution)/shard_map/ppermute | solution.py:235
  99.9 5.6 %collective-permute-done.2.before_ref = bf16[1000,128]{1,0:T(8,128)(2,1)S(1)} collective-permute-done((bf16[1000,128]{1,0:T(8,128)(2,1)S(1)}, bf16[1000,128]{1,0:T(8,128)(2,1)S(1)}, u32[]{:S(2)}, u32[]{:S(2)}) %collective-permute-start.2) | collective-permute-done | bytes 256032 | tf_op jit(solution)/shard_map/ppermute | solution.py:234
  105.5 1.6 %near_sum.3.refs_0_ = f32[1000,256]{1,0:T(8,128)S(1)} custom-call(s32[2,4]{1,0:T(2,128)S(1)} %copy-done.13, s32[2]{0:T(128)S(1)} %copy-done.14, bf16[1000,128]{1,0:T(8,128)(2,1)S(1)} %collective-permute-done.2.before_ref, bf16[1000,256]{1,0:T(8,128)(2,1)S(1)} %get-tuple-element.7.own_ref, bf16[1000,128]{1,0:T(8,128)(2,1)S(1)} %collective-permute-done.3.after_ref, ...), custom_call_target="tpu_custom_call" | custom-call | flops 3000000000 | bytes 3000000 | tf_op jit(solution)/shard_map/near_sum/pallas_call | solution.py:103
  107.1 0.0 copy-start.7
  107.1 1.0 copy-done.7
  108.0 3.5 %all-to-all-done.4.refs_1_ = s16[4,1008,256]{2,1,0:T(8,128)(2,1)S(1)} async-done(((s16[4,1008,256]{2,1,0:T(8,128)(2,1)}), s16[4,1008,256]{2,1,0:T(8,128)(2,1)S(1)}, u32[]{:S(2)}, u32[]{:S(2)}) %all-to-all-start.4) | async-done | bytes 2064416 | tf_op jit(solution)/shard_map/all_to_all | solution.py:222
  111.5 0.0 copy-done.4
  111.5 1.2 %copy-done.8 = f32[1000,256]{1,0:T(8,128)S(1)} copy-done((f32[1000,256]{1,0:T(8,128)S(1)}, f32[1000,256]{1,0:T(8,128)}, u32[]{:S(2)}) %copy-start.8) | copy-done | bytes 1024024
  112.7 1.6 %combine.3 = bf16[1000,256]{1,0:T(8,128)(2,1)} custom-call(f32[1000,256]{1,0:T(8,128)S(1)} %copy-done.8, s16[4,1008,256]{2,1,0:T(8,128)(2,1)S(1)} %all-to-all-done.4.refs_1_, bf16[1000,256]{1,0:T(8,128)(2,1)S(1)} %bitcast.12), custom_call_target="tpu_custom_call" | custom-call | tf_op jit(solution)/shard_map/combine/pallas_call | solution.py:202
  (10 shorter events, 0.1 us)
Async XLA Ops:
  0.0 20.7 %copy-start.2 = (bf16[256,1000]{0,1:T(8,128)(2,1)S(1)}, bf16[256,1000]{0,1:T(8,128)(2,1)}, u32[]{:S(2)}) copy-start(bf16[256,1000]{0,1:T(8,128)(2,1)} %param.9) | copy-start | bytes 1536004
  0.7 1.0 copy-start.9
  1.8 0.7 copy-start.10
  2.4 0.7 copy-start.11
  22.1 17.5 %all-to-all-start.1 = ((bf16[4,1000,256]{2,1,0:T(8,128)(2,1)}), bf16[4,1000,256]{2,1,0:T(8,128)(2,1)S(1)}, u32[]{:S(2)}, u32[]{:S(2)}) async-start(bf16[4,1000,256]{2,1,0:T(8,128)(2,1)} %broadcast_in_dim.2), calls=%async_computation.1 | async-start | bytes 4096000 | tf_op jit(solution)/shard_map/all_to_all | solution.py:222
  42.8 1.3 %copy-start.1 = (s16[4,1008,256]{2,1,0:T(8,128)(2,1)}, s16[4,1008,256]{2,1,0:T(8,128)(2,1)S(1)}, u32[]{:S(2)}) copy-start(s16[4,1008,256]{2,1,0:T(8,128)(2,1)S(1)} %partial_sums.2) | copy-start | bytes 6193156
  44.1 15.8 %copy-start.12 = (bf16[2,4,128,128]{3,2,1,0:T(8,128)(2,1)S(1)}, bf16[2,4,128,128]{3,2,1,0:T(8,128)(2,1)}, u32[]{:S(2)}) copy-start(bf16[2,4,128,128]{3,2,1,0:T(8,128)(2,1)} %tiles_ref.3) | copy-start | bytes 786436
  44.1 15.8 %copy-start.13 = (s32[2,4]{1,0:T(2,128)S(1)}, s32[2,4]{1,0:T(2,128)}, u32[]{:S(2)}) copy-start(s32[2,4]{1,0:T(2,128)} %offset_ref.3) | copy-start | bytes 100
  44.1 15.8 %copy-start.14 = (s32[2]{0:T(128)S(1)}, s32[2]{0:T(128)}, u32[]{:S(2)}) copy-start(s32[2]{0:T(128)} %count_ref.3) | copy-start | bytes 28
  44.1 21.8 %all-to-all-start.2 = ((s16[4,1008,256]{2,1,0:T(8,128)(2,1)}), s16[4,1008,256]{2,1,0:T(8,128)(2,1)S(1)}, u32[]{:S(2)}, u32[]{:S(2)}) async-start(s16[4,1008,256]{2,1,0:T(8,128)(2,1)} %copy-done.1), calls=%async_computation.2 | async-start | bytes 4128768 | tf_op jit(solution)/shard_map/all_to_all | solution.py:222
  50.5 4.9 %collective-permute-start.1 = (bf16[1000,128]{1,0:T(8,128)(2,1)S(1)}, bf16[1000,128]{1,0:T(8,128)(2,1)S(1)}, u32[]{:S(2)}, u32[]{:S(2)}) collective-permute-start(bf16[1000,128]{1,0:T(8,128)(2,1)S(1)} %get-tuple-element.11), channel_id=1, source_target_pairs={{1,0},{2,1},{3,2},{4,3},{5,4},{6,5},{7,6},{8,7},{9,8},{10,9},{11,1... | collective-permute-start | bytes 768008 | tf_op jit(solution)/shard_map/ppermute | solution.py:235
  51.5 8.4 %collective-permute-start = (bf16[1000,128]{1,0:T(8,128)(2,1)S(1)}, bf16[1000,128]{1,0:T(8,128)(2,1)S(1)}, u32[]{:S(2)}, u32[]{:S(2)}) collective-permute-start(bf16[1000,128]{1,0:T(8,128)(2,1)S(1)} %get-tuple-element.12), channel_id=1, source_target_pairs={{0,1},{1,2},{2,3},{3,4},{4,5},{5,6},{6,7},{7,8},{8,9},{9,10},{10,1... | collective-permute-start | bytes 768008 | tf_op jit(solution)/shard_map/ppermute | solution.py:234
  61.5 1.0 copy-start.5
  65.9 1.0 copy-start.3
  67.0 1.2 %copy-start.6 = (f32[1000,256]{1,0:T(8,128)S(1)}, f32[1000,256]{1,0:T(8,128)}, u32[]{:S(2)}) copy-start(f32[1000,256]{1,0:T(8,128)} %copy-done.5) | copy-start | bytes 3072004
  89.6 1.3 %copy-start = (s16[4,1008,256]{2,1,0:T(8,128)(2,1)}, s16[4,1008,256]{2,1,0:T(8,128)(2,1)S(1)}, u32[]{:S(2)}) copy-start(s16[4,1008,256]{2,1,0:T(8,128)(2,1)S(1)} %partial_sums.3) | copy-start | bytes 6193156
  90.9 20.6 %all-to-all-start.4 = ((s16[4,1008,256]{2,1,0:T(8,128)(2,1)}), s16[4,1008,256]{2,1,0:T(8,128)(2,1)S(1)}, u32[]{:S(2)}, u32[]{:S(2)}) async-start(s16[4,1008,256]{2,1,0:T(8,128)(2,1)} %copy-done), calls=%async_computation.4 | async-start | bytes 4128768 | tf_op jit(solution)/shard_map/all_to_all | solution.py:222
  96.0 3.8 %collective-permute-start.3 = (bf16[1000,128]{1,0:T(8,128)(2,1)S(1)}, bf16[1000,128]{1,0:T(8,128)(2,1)S(1)}, u32[]{:S(2)}, u32[]{:S(2)}) collective-permute-start(bf16[1000,128]{1,0:T(8,128)(2,1)S(1)} %get-tuple-element.9), channel_id=1, source_target_pairs={{1,0},{2,1},{3,2},{4,3},{5,4},{6,5},{7,6},{8,7},{9,8},{10,9},{11,1... | collective-permute-start | bytes 768008 | tf_op jit(solution)/shard_map/ppermute | solution.py:235
  96.0 15.5 %copy-start.4 = (bf16[256,1000]{0,1:T(8,128)(2,1)S(1)}, bf16[256,1000]{0,1:T(8,128)(2,1)}, u32[]{:S(2)}) copy-start(bf16[256,1000]{0,1:T(8,128)(2,1)} %param.10) | copy-start | bytes 1536004
  96.1 9.4 %collective-permute-start.2 = (bf16[1000,128]{1,0:T(8,128)(2,1)S(1)}, bf16[1000,128]{1,0:T(8,128)(2,1)S(1)}, u32[]{:S(2)}, u32[]{:S(2)}) collective-permute-start(bf16[1000,128]{1,0:T(8,128)(2,1)S(1)} %get-tuple-element.10), channel_id=1, source_target_pairs={{0,1},{1,2},{2,3},{3,4},{4,5},{5,6},{6,7},{7,8},{8,9},{9,10},{10,1... | collective-permute-start | bytes 768008 | tf_op jit(solution)/shard_map/ppermute | solution.py:234
  107.1 1.0 copy-start.7
  111.5 1.2 %copy-start.8 = (f32[1000,256]{1,0:T(8,128)S(1)}, f32[1000,256]{1,0:T(8,128)}, u32[]{:S(2)}) copy-start(f32[1000,256]{1,0:T(8,128)} %copy-done.7) | copy-start | bytes 3072004

commit v2 on v1

v2 whole, which is shorter than its diff:
```python
import jax
import jax.numpy as jnp
import numpy as np
from jax import lax
from jax.experimental import pallas as pl
from jax.experimental.pallas import tpu as pltpu
from jax.sharding import Mesh, PartitionSpec as P

SWEEPS = 2
SIDE = 4
PEERS = 4
PARTNERS = (3, 1, 2)
CODE_ROWS = 16
CODE_BITS = 13
CHUNK = 112
POWER_ROWS = 8

propagation_weight = 0.9
epsilon = 1e-06

VMEM = pl.BlockSpec(memory_space=pltpu.VMEM)
SMEM = pl.BlockSpec(memory_space=pltpu.SMEM)
MIB = 1024 * 1024


def squares(shift):
    return [
        [((2 * i + k - shift) % SIDE) * SIDE + (2 * j + m - shift) % SIDE for k in (0, 1) for m in (0, 1)]
        for i in (0, 1)
        for j in (0, 1)
    ]


def partner_table(core, phase):
    table = {}
    for square in squares((core + phase) % 2):
        for place, chip in enumerate(square):
            table[chip] = [square[place ^ s] for s in range(PEERS)]
    return table


def partner_pairs(inner, phase, s):
    return [
        (chip * inner + pos, partner_table(pos % 2, phase)[chip][s] * inner + pos)
        for pos in range(inner)
        for chip in range(SIDE * SIDE)
    ]


def square_groups(inner, phase):
    return [
        [chip * inner + pos for chip in square] for pos in range(inner) for square in squares((pos + phase) % 2)
    ]


def tile_order():
    order = np.zeros((2, SIDE * SIDE, PEERS, PEERS), np.int32)
    for core in range(2):
        first = partner_table(core, 0)
        for square in squares((core + 1) % 2):
            for chip in square:
                for b, middle in enumerate(square):
                    order[core, chip, b] = first[middle]
    return order


def pack_kernel(order_ref, row_ref, block_ref, tiles_ref, out_ref):
    size = tiles_ref.shape[-1]
    blocks = 2
    for b in range(PEERS):
        sublane = lax.broadcasted_iota(jnp.int32, (CODE_ROWS, size), 0)
        codes = jnp.zeros((CODE_ROWS, size), jnp.float32)
        for a in range(PEERS):
            q = order_ref[b, a]
            out_ref[b, a * size : (a + 1) * size, :] = tiles_ref[q]
            code = (row_ref[q] * blocks + block_ref[q]).astype(jnp.float32)
            codes = jnp.where(sublane == a, code, codes)
        out_ref[b, PEERS * size :, :] = codes.astype(jnp.bfloat16)


def pack(order, row, block, tiles):
    size = tiles.shape[-1]
    return pl.pallas_call(
        pack_kernel,
        out_shape=jax.ShapeDtypeStruct((PEERS, PEERS * size + CODE_ROWS, size), jnp.bfloat16),
        in_specs=[SMEM, SMEM, SMEM, VMEM],
        out_specs=VMEM,
        compiler_params=pltpu.CompilerParams(vmem_limit_bytes=4 * MIB),
        name="pack",
    )(order, row, block, tiles)


def times_transposed(left, right):
    return lax.dot_general(left, right, (((1,), (1,)), ((), ())), preferred_element_type=jnp.float32)


def fill(code_ref, d, source_refs, tiles_ref, left, right):
    size = tiles_ref.shape[-1]
    for a, source_ref in enumerate(source_refs):
        code = code_ref[d, a]
        tile = tiles_ref[d, a * size : (a + 1) * size, :]
        for r in range(2):
            right[r * size : (r + 1) * size, a * size : (a + 1) * size] = jnp.where(
                code // 2 == r, tile, jnp.zeros_like(tile)
            )
        lane = pl.multiple_of((code % 2) * size, size)
        left[:, a * size : (a + 1) * size] = source_ref[:, pl.ds(lane, size)]


def near_kernel(core_ref, offset_ref, count_ref, own_ref, even_ref, odd_ref, tiles_ref, sum_ref, ext, left, right):
    blocks, slots, size, _ = tiles_ref.shape

    @pl.when(core_ref[0] == 0)
    def _():
        ext[0] = odd_ref[:, size:]
        ext[blocks + 1] = even_ref[:, :size]

    @pl.when(core_ref[0] != 0)
    def _():
        ext[0] = even_ref[:, size:]
        ext[blocks + 1] = odd_ref[:, :size]

    for b in range(blocks):
        ext[b + 1] = own_ref[:, b * size : (b + 1) * size]
    for b in range(blocks):
        for s in range(slots):
            tile = tiles_ref[b, s]
            right[:, s * size : (s + 1) * size] = jnp.where(s < count_ref[b], tile, jnp.zeros_like(tile))
            left[:, s * size : (s + 1) * size] = ext[b + 1 + offset_ref[b, s]]
        sum_ref[:, b * size : (b + 1) * size] = times_transposed(left[...], right[...])


def near_sum(core, offset, count, own, even, odd, tiles):
    blocks, slots, size, _ = tiles.shape
    classes, width = even.shape
    return pl.pallas_call(
        near_kernel,
        out_shape=jax.ShapeDtypeStruct((classes, width), jnp.float32),
        in_specs=[SMEM] * 3 + [VMEM] * 4,
        out_specs=VMEM,
        scratch_shapes=[
            pltpu.VMEM((blocks + 2, classes, size), jnp.bfloat16),
            pltpu.VMEM((classes, slots * size), jnp.bfloat16),
            pltpu.VMEM((size, slots * size), jnp.bfloat16),
        ],
        cost_estimate=pl.CostEstimate(flops=3_000_000_000, bytes_accessed=3_000_000, transcendentals=0),
        compiler_params=pltpu.CompilerParams(vmem_limit_bytes=12 * MIB),
        name="near_sum",
    )(core, offset, count, own, even, odd, tiles)


def partial_kernel(code_ref, *refs):
    source_refs, (tiles_ref, out_ref, left, right, acc) = refs[:PEERS], refs[PEERS:]
    classes, width = source_refs[0].shape
    height = out_ref.shape[1]
    acc[classes:, :] = jnp.zeros((height - classes, width), jnp.float32)

    for d in range(PEERS):
        fill(code_ref, d, source_refs, tiles_ref, left, right)
        acc[:classes, :] = times_transposed(left[...], right[...])
        peak = jnp.max(jnp.abs(acc[...]), axis=0, keepdims=True)
        power = jnp.floor(jnp.log2(jnp.maximum(peak, 1e-30)))
        scale = jnp.exp2(CODE_BITS - power)
        for at in range(0, height, CHUNK):
            scaled = jnp.round(acc[at : at + CHUNK, :] * scale)
            if at + CHUNK > classes:
                sublane = lax.broadcasted_iota(jnp.int32, scaled.shape, 0) + at
                scaled = jnp.where(sublane < classes, scaled, power)
            out_ref[d, at : at + CHUNK, :] = scaled.astype(jnp.int32).astype(jnp.int16)


def partial_sums(code, sources, tiles):
    classes, width = sources[0].shape
    size = tiles.shape[-1]
    height = classes + POWER_ROWS
    return pl.pallas_call(
        partial_kernel,
        out_shape=jax.ShapeDtypeStruct((PEERS, height, width), jnp.int16),
        in_specs=[SMEM] + [VMEM] * (PEERS + 1),
        out_specs=VMEM,
        scratch_shapes=[
            pltpu.VMEM((classes, PEERS * size), jnp.bfloat16),
            pltpu.VMEM((width, PEERS * size), jnp.bfloat16),
            pltpu.VMEM((height, width), jnp.float32),
        ],
        cost_estimate=pl.CostEstimate(flops=500_000_000, bytes_accessed=3_000_000, transcendentals=0),
        compiler_params=pltpu.CompilerParams(vmem_limit_bytes=12 * MIB),
        name="partial_sums",
    )(code, *sources, tiles)


def combine_kernel(near_ref, affinity_ref, parts_ref, out_ref, mixed_ref):
    classes, width = near_ref.shape
    power_at = classes - POWER_ROWS
    scales = []
    for p in range(PEERS):
        power = parts_ref[p, power_at:, :].astype(jnp.int32).astype(jnp.float32)[POWER_ROWS : POWER_ROWS + 1, :]
        scales.append(jnp.exp2(power - CODE_BITS))
    square = jnp.zeros((1, width), jnp.float32)
    for start in range(0, classes, CHUNK):
        at = slice(start, min(start + CHUNK, classes))
        total = near_ref[at, :]
        for p in range(PEERS):
            total += parts_ref[p, at, :].astype(jnp.int32).astype(jnp.float32) * scales[p]
        mixed = propagation_weight * total + affinity_ref[at, :].astype(jnp.float32)
        mixed_ref[at, :] = mixed
        square += jnp.sum(mixed * mixed, axis=0, keepdims=True)
    row_scale = lax.rsqrt(square * (1.0 / classes) + epsilon)
    for start in range(0, classes, CHUNK):
        at = slice(start, min(start + CHUNK, classes))
        out_ref[at, :] = (mixed_ref[at, :] * row_scale).astype(jnp.bfloat16)


def combine(near, affinity, parts):
    return pl.pallas_call(
        combine_kernel,
        out_shape=jax.ShapeDtypeStruct(near.shape, jnp.bfloat16),
        in_specs=[VMEM] * 3,
        out_specs=VMEM,
        scratch_shapes=[pltpu.VMEM(near.shape, jnp.float32)],
        cost_estimate=pl.CostEstimate(flops=1_000_000_000, bytes_accessed=3_000_000, transcendentals=0),
        compiler_params=pltpu.CompilerParams(vmem_limit_bytes=8 * MIB),
        name="combine",
    )(near, affinity, parts)


def local(inner, posterior, class_affinity, band_tiles, band_offset, band_count, far_tiles, far_row, far_block):
    size = band_tiles.shape[2]
    chips = SIDE * SIDE
    device = lax.axis_index("d")
    core, chip = (device % inner) % 2, device // inner
    order = jnp.asarray(tile_order())[core, chip]
    core = core.reshape(1)
    even = [(x * inner + j, x * inner + (j ^ 1)) for x in range(chips) for j in range(inner)]
    odd = [(x * inner + j, x * inner + (j + (1 if j % 2 else -1)) % inner) for x in range(chips) for j in range(inner)]

    def swap(value, phase, s):
        return lax.ppermute(value, "d", partner_pairs(inner, phase, s))

    current = posterior.T
    affinity = class_affinity.T
    for sweep in range(SWEEPS):
        sources = [current] + [None] * len(PARTNERS)
        for s in PARTNERS:
            sources[s] = swap(current, 0, s)
        if sweep == 0:
            payload = lax.all_to_all(
                pack(order, far_row.reshape(chips), far_block.reshape(chips), far_tiles.reshape(chips, size, size)),
                "d", 0, 0, tiled=True, axis_index_groups=square_groups(inner, 1),
            )
            code = payload[:, PEERS * size : PEERS * size + PEERS, 0].astype(jnp.int32)
        from_even = lax.ppermute(current, "d", even)
        from_odd = lax.ppermute(current, "d", odd)
        near = near_sum(core, band_offset, band_count, current, from_even, from_odd, band_tiles)
        part = partial_sums(code, sources, payload)
        parts = lax.all_to_all(part, "d", 0, 0, tiled=True, axis_index_groups=square_groups(inner, 1))
        current = combine(near, affinity, parts)
    return current.T


def solution(mesh):
    inner = mesh.shape["gy"]
    flat = Mesh(mesh.devices.reshape(-1), ("d",))
    spec = P("d")
    return jax.shard_map(
        lambda *args: local(inner, *args), mesh=flat, in_specs=(spec,) * 8, out_specs=spec, check_vma=False
    )
```

time: 115 us -> 120 us (1.043)
  the two profiles are of different devices: /device:TPU:6 before, /device:TPU:1 now
where the time goes in v2:
time: 120 us; the launch traced here: 119 us
  starting transfers between devices  54.3 us (45%)
  waiting for transfers between devices  38.5 us (32%)
  Pallas kernels  14.4 us (12%)
  local copies, waits for them, and re-layouts  11.6 us (10%)
    ppermute x6, starting transfers between devices, swap(): return lax.ppermute(value, 'd', partner_pairs(inner, phase, s))  22.4 us
    ppermute x6, waiting for transfers between devices, swap(): return lax.ppermute(value, 'd', partner_pairs(inner, phase, s))  20.9 us
    ppermute x2, waiting for transfers between devices, local(): from_odd = lax.ppermute(current, 'd', odd)  17.7 us
    ppermute x2, starting transfers between devices, local(): from_even = lax.ppermute(current, 'd', even)  16.4 us
    unnamed x32, local copies, waits for them, and re-layouts  10.9 us
    all_to_all x2, starting transfers between devices, local(): lax.all_to_all(part, 'd', 0, 0, tiled=True, axis_index_groups=square_grou...  7.34 us
    pallas_call x2, Pallas kernels, partial_sums(): pl.pallas_call(partial_kernel, out_shape=jax.ShapeDtypeStruct((PEERS, hei...  7.29 us
    all_to_all x1, starting transfers between devices, local(): lax.all_to_all(pack(order, far_row.reshape(chips), far_block.reshape(chip...  4.31 us
  transfers between devices with their start and end apart: 13, of which 6 were waited for; matrix products, arithmetic and copies ran while one was open for 0% of the time, Pallas kernels for 3%

profile of v2, /device:TPU:1, one launch (start us, length us, event | category | flops | bytes accessed | tf_op | source)
XLA Modules:
  0.0 119.3 jit_solution(18391955937056964699)
XLA Ops:
  0.0 0.7 dynamic-slice_bitcast_fusion.order_ref
  0.7 1.0 copy-done.8
  1.7 0.7 copy-done.11
  2.4 0.7 copy-done.12
  3.0 1.4 %pack.1 = bf16[4,528,128]{2,1,0:T(8,128)(2,1)} custom-call(s32[4,4]{1,0:T(4,128)S(1)} %dynamic-slice_bitcast_fusion.order_ref, s32[16]{0:T(128)S(1)} %bitcast.19, s32[16]{0:T(128)S(1)} %bitcast.20, bf16[16,128,128]{2,1,0:T(8,128)(2,1)S(1)} %bitcast.11), custom_call_target="tpu_custom_call" | custom-call | tf_op jit(solution)/shard_map/pack/pallas_call | solution.py:83
  4.5 4.3 %all-to-all-start = ((bf16[4,528,128]{2,1,0:T(8,128)(2,1)}), bf16[4,528,128]{2,1,0:T(8,128)(2,1)S(1)}, u32[]{:S(2)}, u32[]{:S(2)}) async-start(bf16[4,528,128]{2,1,0:T(8,128)(2,1)} %pack.1), calls=%async_computation | async-start | bytes 1081344 | tf_op jit(solution)/shard_map/all_to_all | solution.py:247
  8.8 0.0 copy-done.9
  8.8 4.9 %collective-permute-start.2 = (bf16[1000,256]{1,0:T(8,128)(2,1)S(1)}, bf16[1000,256]{1,0:T(8,128)(2,1)S(1)}, u32[]{:S(2)}, u32[]{:S(2)}) collective-permute-start(bf16[1000,256]{1,0:T(8,128)(2,1)S(1)} %bitcast.12), channel_id=1, source_target_pairs={{0,32},{32,0},{64,96},{96,64},{128,160},{160,128},{192,224},{224,1... | collective-permute-start | bytes 1536008 | tf_op jit(solution)/shard_map/ppermute | solution.py:238
  13.7 4.8 %collective-permute-start.3 = (bf16[1000,256]{1,0:T(8,128)(2,1)S(1)}, bf16[1000,256]{1,0:T(8,128)(2,1)S(1)}, u32[]{:S(2)}, u32[]{:S(2)}) collective-permute-start(bf16[1000,256]{1,0:T(8,128)(2,1)S(1)} %bitcast.13), channel_id=1, source_target_pairs={{0,128},{32,160},{64,192},{96,224},{128,0},{160,32},{192,64},{224,... | collective-permute-start | bytes 1536008 | tf_op jit(solution)/shard_map/ppermute | solution.py:238
  18.5 1.9 %collective-permute-start.4 = (bf16[1000,256]{1,0:T(8,128)(2,1)S(1)}, bf16[1000,256]{1,0:T(8,128)(2,1)S(1)}, u32[]{:S(2)}, u32[]{:S(2)}) collective-permute-start(bf16[1000,256]{1,0:T(8,128)(2,1)S(1)} %bitcast.14), channel_id=1, source_target_pairs={{0,160},{32,128},{64,224},{96,192},{128,32},{160,0},{192,96},{224,... | collective-permute-start | bytes 1536008 | tf_op jit(solution)/shard_map/ppermute | solution.py:238
  20.4 0.0 all-to-all-done.refs_4_
  20.4 0.1 convert_reduce_fusion.code_ref
  20.6 0.3 collective-permute-done.2.refs_1_
  20.9 12.5 %collective-permute-done.3.refs_2_ = bf16[1000,256]{1,0:T(8,128)(2,1)S(1)} collective-permute-done((bf16[1000,256]{1,0:T(8,128)(2,1)S(1)}, bf16[1000,256]{1,0:T(8,128)(2,1)S(1)}, u32[]{:S(2)}, u32[]{:S(2)}) %collective-permute-start.3) | collective-permute-done | bytes 512032 | tf_op jit(solution)/shard_map/ppermute | solution.py:238
  33.5 0.0 collective-permute-done.4.refs_3_
  33.5 2.9 %partial_sums.2 = s16[4,1008,256]{2,1,0:T(8,128)(2,1)S(1)} custom-call(s32[4,4]{1,0:T(4,128)S(1)} %convert_reduce_fusion.code_ref, bf16[1000,256]{1,0:T(8,128)(2,1)S(1)} %bitcast.15, bf16[1000,256]{1,0:T(8,128)(2,1)S(1)} %collective-permute-done.2.refs_1_, bf16[1000,256]{1,0:T(8,128)(2,1)S(1)} %collective-permute-done.3.refs_2_, ...), custom_call_target="tpu_custom_call" | custom-call | flops 500000000 | bytes 3000000 | tf_op jit(solution)/shard_map/partial_sums/pallas_call | solution.py:176
  36.4 1.3 %copy-done = s16[4,1008,256]{2,1,0:T(8,128)(2,1)} copy-done((s16[4,1008,256]{2,1,0:T(8,128)(2,1)}, s16[4,1008,256]{2,1,0:T(8,128)(2,1)S(1)}, u32[]{:S(2)}) %copy-start) | copy-done | bytes 2064408
  37.7 3.7 %all-to-all-start.1 = ((s16[4,1008,256]{2,1,0:T(8,128)(2,1)}), s16[4,1008,256]{2,1,0:T(8,128)(2,1)S(1)}, u32[]{:S(2)}, u32[]{:S(2)}) async-start(s16[4,1008,256]{2,1,0:T(8,128)(2,1)} %copy-done), calls=%async_computation.1 | async-start | bytes 4128768 | tf_op jit(solution)/shard_map/all_to_all | solution.py:256
  41.4 7.7 %collective-permute-start = (bf16[1000,256]{1,0:T(8,128)(2,1)S(1)}, bf16[1000,256]{1,0:T(8,128)(2,1)S(1)}, u32[]{:S(2)}, u32[]{:S(2)}) collective-permute-start(bf16[1000,256]{1,0:T(8,128)(2,1)S(1)} %bitcast.16), channel_id=1, source_target_pairs={{0,1},{1,0},{2,3},{3,2},{4,5},{5,4},{6,7},{7,6},{8,9},{9,8},{10,11... | collective-permute-start | bytes 1536008 | tf_op jit(solution)/shard_map/ppermute | solution.py:252
  49.2 1.9 %collective-permute-start.1 = (bf16[1000,256]{1,0:T(8,128)(2,1)S(1)}, bf16[1000,256]{1,0:T(8,128)(2,1)S(1)}, u32[]{:S(2)}, u32[]{:S(2)}) collective-permute-start(bf16[1000,256]{1,0:T(8,128)(2,1)S(1)} %bitcast.17), channel_id=1, source_target_pairs={{0,31},{1,2},{2,1},{3,4},{4,3},{5,6},{6,5},{7,8},{8,7},{9,10},{10,... | collective-permute-start | bytes 1536008 | tf_op jit(solution)/shard_map/ppermute | solution.py:253
  51.1 0.0 collective-permute-done.even_ref
  51.1 8.7 %collective-permute-done.1.odd_ref = bf16[1000,256]{1,0:T(8,128)(2,1)S(1)} collective-permute-done((bf16[1000,256]{1,0:T(8,128)(2,1)S(1)}, bf16[1000,256]{1,0:T(8,128)(2,1)S(1)}, u32[]{:S(2)}, u32[]{:S(2)}) %collective-permute-start.1) | collective-permute-done | bytes 512032 | tf_op jit(solution)/shard_map/ppermute | solution.py:253
  59.8 0.0 copy-start.10
  59.9 1.0 copy-done.10
  60.9 1.7 %near_sum.2.near_ref = f32[1000,256]{1,0:T(8,128)S(1)} custom-call(s32[1]{0:T(128)} %bitcast.core_ref, s32[2,4]{1,0:T(2,128)S(1)} %copy-done.14, s32[2]{0:T(128)S(1)} %copy-done.15, bf16[1000,256]{1,0:T(8,128)(2,1)S(1)} %bitcast.18, bf16[1000,256]{1,0:T(8,128)(2,1)S(1)} %collective-permute-done.even_ref, ...), custom_call_target="tpu_custom_call" | custom-call | flops 3000000000 | bytes 3000000 | tf_op jit(solution)/shard_map/near_sum/pallas_call | solution.py:136
  62.6 1.0 copy-done.6
  63.5 0.0 all-to-all-done.1.parts_ref
  63.5 1.2 %copy-done.7 = f32[1000,256]{1,0:T(8,128)S(1)} copy-done((f32[1000,256]{1,0:T(8,128)S(1)}, f32[1000,256]{1,0:T(8,128)}, u32[]{:S(2)}) %copy-start.7) | copy-done | bytes 1024024
  64.8 0.8 combine.2.own_ref.refs_0_
  65.5 2.2 %collective-permute-start.7 = (bf16[1000,256]{1,0:T(8,128)(2,1)S(1)}, bf16[1000,256]{1,0:T(8,128)(2,1)S(1)}, u32[]{:S(2)}, u32[]{:S(2)}) collective-permute-start(bf16[1000,256]{1,0:T(8,128)(2,1)S(1)} %combine.2.own_ref.refs_0_), channel_id=1, source_target_pairs={{0,32},{32,0},{64,96},{96,64},{128,160},{160,128},{192,224},{224,1... | collective-permute-start | bytes 1536008 | tf_op jit(solution)/shard_map/ppermute | solution.py:238
  67.7 1.9 %collective-permute-start.8 = (bf16[1000,256]{1,0:T(8,128)(2,1)S(1)}, bf16[1000,256]{1,0:T(8,128)(2,1)S(1)}, u32[]{:S(2)}, u32[]{:S(2)}) collective-permute-start(bf16[1000,256]{1,0:T(8,128)(2,1)S(1)} %combine.2.own_ref.refs_0_), channel_id=1, source_target_pairs={{0,128},{32,160},{64,192},{96,224},{128,0},{160,32},{192,64},{224,... | collective-permute-start | bytes 1536008 | tf_op jit(solution)/shard_map/ppermute | solution.py:238
  69.7 6.7 %collective-permute-start.9 = (bf16[1000,256]{1,0:T(8,128)(2,1)S(1)}, bf16[1000,256]{1,0:T(8,128)(2,1)S(1)}, u32[]{:S(2)}, u32[]{:S(2)}) collective-permute-start(bf16[1000,256]{1,0:T(8,128)(2,1)S(1)} %combine.2.own_ref.refs_0_), channel_id=1, source_target_pairs={{0,160},{32,128},{64,224},{96,192},{128,32},{160,0},{192,96},{224,... | collective-permute-start | bytes 1536008 | tf_op jit(solution)/shard_map/ppermute | solution.py:238
  76.4 0.2 collective-permute-done.7.refs_1_
  76.6 7.8 %collective-permute-done.8.refs_2_ = bf16[1000,256]{1,0:T(8,128)(2,1)S(1)} collective-permute-done((bf16[1000,256]{1,0:T(8,128)(2,1)S(1)}, bf16[1000,256]{1,0:T(8,128)(2,1)S(1)}, u32[]{:S(2)}, u32[]{:S(2)}) %collective-permute-start.8) | collective-permute-done | bytes 512032 | tf_op jit(solution)/shard_map/ppermute | solution.py:238
  84.4 0.0 collective-permute-done.9.refs_3_
  84.4 4.4 %partial_sums.3 = s16[4,1008,256]{2,1,0:T(8,128)(2,1)} custom-call(s32[4,4]{1,0:T(4,128)S(1)} %convert_reduce_fusion.code_ref, bf16[1000,256]{1,0:T(8,128)(2,1)S(1)} %combine.2.own_ref.refs_0_, bf16[1000,256]{1,0:T(8,128)(2,1)S(1)} %collective-permute-done.7.refs_1_, bf16[1000,256]{1,0:T(8,128)(2,1)S(1)} %collective-permute-done.8.refs_2_, ...), custom_call_target="tpu_custom_call" | custom-call | flops 500000000 | bytes 3000000 | tf_op jit(solution)/shard_map/partial_sums/pallas_call | solution.py:176
  88.8 0.8 copy-done.2
  89.6 3.6 %all-to-all-start.2 = ((s16[4,1008,256]{2,1,0:T(8,128)(2,1)}), s16[4,1008,256]{2,1,0:T(8,128)(2,1)S(1)}, u32[]{:S(2)}, u32[]{:S(2)}) async-start(s16[4,1008,256]{2,1,0:T(8,128)(2,1)} %partial_sums.3), calls=%async_computation.2 | async-start | bytes 4128768 | tf_op jit(solution)/shard_map/all_to_all | solution.py:256
  93.2 8.7 %collective-permute-start.5 = (bf16[1000,256]{1,0:T(8,128)(2,1)}, bf16[1000,256]{1,0:T(8,128)(2,1)S(1)}, u32[]{:S(2)}, u32[]{:S(2)}) collective-permute-start(bf16[1000,256]{1,0:T(8,128)(2,1)} %copy-done.2), channel_id=1, source_target_pairs={{0,1},{1,0},{2,3},{3,2},{4,5},{5,4},{6,7},{7,6},{8,9},{9,8},{10,11... | collective-permute-start | bytes 1536008 | tf_op jit(solution)/shard_map/ppermute | solution.py:252
  101.9 1.9 %collective-permute-start.6 = (bf16[1000,256]{1,0:T(8,128)(2,1)}, bf16[1000,256]{1,0:T(8,128)(2,1)S(1)}, u32[]{:S(2)}, u32[]{:S(2)}) collective-permute-start(bf16[1000,256]{1,0:T(8,128)(2,1)} %copy-done.2), channel_id=1, source_target_pairs={{0,31},{1,2},{2,1},{3,4},{4,3},{5,6},{6,5},{7,8},{8,7},{9,10},{10,... | collective-permute-start | bytes 1536008 | tf_op jit(solution)/shard_map/ppermute | solution.py:253
  103.8 0.0 collective-permute-done.5.even_ref
  103.8 8.9 %collective-permute-done.6.odd_ref = bf16[1000,256]{1,0:T(8,128)(2,1)S(1)} collective-permute-done((bf16[1000,256]{1,0:T(8,128)(2,1)}, bf16[1000,256]{1,0:T(8,128)(2,1)S(1)}, u32[]{:S(2)}, u32[]{:S(2)}) %collective-permute-start.6) | collective-permute-done | bytes 512032 | tf_op jit(solution)/shard_map/ppermute | solution.py:253
  112.8 1.0 copy-done.3
  113.8 1.7 %near_sum.3.near_ref = f32[1000,256]{1,0:T(8,128)S(1)} custom-call(s32[1]{0:T(128)} %bitcast.core_ref, s32[2,4]{1,0:T(2,128)S(1)} %copy-done.14, s32[2]{0:T(128)S(1)} %copy-done.15, bf16[1000,256]{1,0:T(8,128)(2,1)S(1)} %copy-done.3, bf16[1000,256]{1,0:T(8,128)(2,1)S(1)} %collective-permute-done.5.even_ref, ...), custom_call_target="tpu_custom_call" | custom-call | flops 3000000000 | bytes 3000000 | tf_op jit(solution)/shard_map/near_sum/pallas_call | solution.py:136
  115.5 1.0 copy-done.4
  116.5 0.0 all-to-all-done.2.parts_ref
  116.5 1.2 %copy-done.5 = f32[1000,256]{1,0:T(8,128)S(1)} copy-done((f32[1000,256]{1,0:T(8,128)S(1)}, f32[1000,256]{1,0:T(8,128)}, u32[]{:S(2)}) %copy-start.5) | copy-done | bytes 1024024
  117.7 1.6 %combine.3 = bf16[1000,256]{1,0:T(8,128)(2,1)} custom-call(f32[1000,256]{1,0:T(8,128)S(1)} %copy-done.5, bf16[1000,256]{1,0:T(8,128)(2,1)S(1)} %bitcast.10, s16[4,1008,256]{2,1,0:T(8,128)(2,1)S(1)} %all-to-all-done.2.parts_ref), custom_call_target="tpu_custom_call" | custom-call | flops 1000000000 | bytes 3000000 | tf_op jit(solution)/shard_map/combine/pallas_call | solution.py:215
  (19 shorter events, 0.0 us)
Async XLA Ops:
  0.7 1.0 copy-start.8
  1.7 0.7 copy-start.11
  2.4 0.7 copy-start.12
  3.0 5.8 %copy-start.9 = (bf16[256,1000]{0,1:T(8,128)(2,1)S(1)}, bf16[256,1000]{0,1:T(8,128)(2,1)}, u32[]{:S(2)}) copy-start(bf16[256,1000]{0,1:T(8,128)(2,1)} %param.9) | copy-start | bytes 1536004
  4.5 16.0 %all-to-all-start = ((bf16[4,528,128]{2,1,0:T(8,128)(2,1)}), bf16[4,528,128]{2,1,0:T(8,128)(2,1)S(1)}, u32[]{:S(2)}, u32[]{:S(2)}) async-start(bf16[4,528,128]{2,1,0:T(8,128)(2,1)} %pack.1), calls=%async_computation | async-start | bytes 1081344 | tf_op jit(solution)/shard_map/all_to_all | solution.py:247
  8.8 12.1 %collective-permute-start.2 = (bf16[1000,256]{1,0:T(8,128)(2,1)S(1)}, bf16[1000,256]{1,0:T(8,128)(2,1)S(1)}, u32[]{:S(2)}, u32[]{:S(2)}) collective-permute-start(bf16[1000,256]{1,0:T(8,128)(2,1)S(1)} %bitcast.12), channel_id=1, source_target_pairs={{0,32},{32,0},{64,96},{96,64},{128,160},{160,128},{192,224},{224,1... | collective-permute-start | bytes 1536008 | tf_op jit(solution)/shard_map/ppermute | solution.py:238
  13.7 19.8 %collective-permute-start.3 = (bf16[1000,256]{1,0:T(8,128)(2,1)S(1)}, bf16[1000,256]{1,0:T(8,128)(2,1)S(1)}, u32[]{:S(2)}, u32[]{:S(2)}) collective-permute-start(bf16[1000,256]{1,0:T(8,128)(2,1)S(1)} %bitcast.13), channel_id=1, source_target_pairs={{0,128},{32,160},{64,192},{96,224},{128,0},{160,32},{192,64},{224,... | collective-permute-start | bytes 1536008 | tf_op jit(solution)/shard_map/ppermute | solution.py:238
  18.5 14.9 %collective-permute-start.4 = (bf16[1000,256]{1,0:T(8,128)(2,1)S(1)}, bf16[1000,256]{1,0:T(8,128)(2,1)S(1)}, u32[]{:S(2)}, u32[]{:S(2)}) collective-permute-start(bf16[1000,256]{1,0:T(8,128)(2,1)S(1)} %bitcast.14), channel_id=1, source_target_pairs={{0,160},{32,128},{64,224},{96,192},{128,32},{160,0},{192,96},{224,... | collective-permute-start | bytes 1536008 | tf_op jit(solution)/shard_map/ppermute | solution.py:238
  36.4 1.3 %copy-start = (s16[4,1008,256]{2,1,0:T(8,128)(2,1)}, s16[4,1008,256]{2,1,0:T(8,128)(2,1)S(1)}, u32[]{:S(2)}) copy-start(s16[4,1008,256]{2,1,0:T(8,128)(2,1)S(1)} %partial_sums.2) | copy-start | bytes 6193156
  37.7 22.1 %copy-start.13 = (bf16[2,4,128,128]{3,2,1,0:T(8,128)(2,1)S(1)}, bf16[2,4,128,128]{3,2,1,0:T(8,128)(2,1)}, u32[]{:S(2)}) copy-start(bf16[2,4,128,128]{3,2,1,0:T(8,128)(2,1)} %tiles_ref.3) | copy-start | bytes 786436
  37.7 22.1 %copy-start.14 = (s32[2,4]{1,0:T(2,128)S(1)}, s32[2,4]{1,0:T(2,128)}, u32[]{:S(2)}) copy-start(s32[2,4]{1,0:T(2,128)} %offset_ref.3) | copy-start | bytes 100
  37.7 22.1 %copy-start.15 = (s32[2]{0:T(128)S(1)}, s32[2]{0:T(128)}, u32[]{:S(2)}) copy-start(s32[2]{0:T(128)} %count_ref.3) | copy-start | bytes 28
  37.7 25.8 %all-to-all-start.1 = ((s16[4,1008,256]{2,1,0:T(8,128)(2,1)}), s16[4,1008,256]{2,1,0:T(8,128)(2,1)S(1)}, u32[]{:S(2)}, u32[]{:S(2)}) async-start(s16[4,1008,256]{2,1,0:T(8,128)(2,1)} %copy-done), calls=%async_computation.1 | async-start | bytes 4128768 | tf_op jit(solution)/shard_map/all_to_all | solution.py:256
  41.4 9.7 %collective-permute-start = (bf16[1000,256]{1,0:T(8,128)(2,1)S(1)}, bf16[1000,256]{1,0:T(8,128)(2,1)S(1)}, u32[]{:S(2)}, u32[]{:S(2)}) collective-permute-start(bf16[1000,256]{1,0:T(8,128)(2,1)S(1)} %bitcast.16), channel_id=1, source_target_pairs={{0,1},{1,0},{2,3},{3,2},{4,5},{5,4},{6,7},{7,6},{8,9},{9,8},{10,11... | collective-permute-start | bytes 1536008 | tf_op jit(solution)/shard_map/ppermute | solution.py:252
  49.2 10.7 %collective-permute-start.1 = (bf16[1000,256]{1,0:T(8,128)(2,1)S(1)}, bf16[1000,256]{1,0:T(8,128)(2,1)S(1)}, u32[]{:S(2)}, u32[]{:S(2)}) collective-permute-start(bf16[1000,256]{1,0:T(8,128)(2,1)S(1)} %bitcast.17), channel_id=1, source_target_pairs={{0,31},{1,2},{2,1},{3,4},{4,3},{5,6},{6,5},{7,8},{8,7},{9,10},{10,... | collective-permute-start | bytes 1536008 | tf_op jit(solution)/shard_map/ppermute | solution.py:253
  59.8 1.0 copy-start.10
  60.9 2.7 %copy-start.1 = (bf16[256,1000]{0,1:T(8,128)(2,1)S(1)}, bf16[256,1000]{0,1:T(8,128)(2,1)}, u32[]{:S(2)}) copy-start(bf16[256,1000]{0,1:T(8,128)(2,1)} %param.10) | copy-start | bytes 1536004
  62.5 1.0 copy-start.6
  63.5 1.2 %copy-start.7 = (f32[1000,256]{1,0:T(8,128)S(1)}, f32[1000,256]{1,0:T(8,128)}, u32[]{:S(2)}) copy-start(f32[1000,256]{1,0:T(8,128)} %copy-done.6) | copy-start | bytes 3072004
  65.5 11.0 %collective-permute-start.7 = (bf16[1000,256]{1,0:T(8,128)(2,1)S(1)}, bf16[1000,256]{1,0:T(8,128)(2,1)S(1)}, u32[]{:S(2)}, u32[]{:S(2)}) collective-permute-start(bf16[1000,256]{1,0:T(8,128)(2,1)S(1)} %combine.2.own_ref.refs_0_), channel_id=1, source_target_pairs={{0,32},{32,0},{64,96},{96,64},{128,160},{160,128},{192,224},{224,1... | collective-permute-start | bytes 1536008 | tf_op jit(solution)/shard_map/ppermute | solution.py:238
  67.7 16.6 %collective-permute-start.8 = (bf16[1000,256]{1,0:T(8,128)(2,1)S(1)}, bf16[1000,256]{1,0:T(8,128)(2,1)S(1)}, u32[]{:S(2)}, u32[]{:S(2)}) collective-permute-start(bf16[1000,256]{1,0:T(8,128)(2,1)S(1)} %combine.2.own_ref.refs_0_), channel_id=1, source_target_pairs={{0,128},{32,160},{64,192},{96,224},{128,0},{160,32},{192,64},{224,... | collective-permute-start | bytes 1536008 | tf_op jit(solution)/shard_map/ppermute | solution.py:238
  69.7 14.7 %collective-permute-start.9 = (bf16[1000,256]{1,0:T(8,128)(2,1)S(1)}, bf16[1000,256]{1,0:T(8,128)(2,1)S(1)}, u32[]{:S(2)}, u32[]{:S(2)}) collective-permute-start(bf16[1000,256]{1,0:T(8,128)(2,1)S(1)} %combine.2.own_ref.refs_0_), channel_id=1, source_target_pairs={{0,160},{32,128},{64,224},{96,192},{128,32},{160,0},{192,96},{224,... | collective-permute-start | bytes 1536008 | tf_op jit(solution)/shard_map/ppermute | solution.py:238
  88.8 0.8 copy-start.2
  89.6 26.9 %all-to-all-start.2 = ((s16[4,1008,256]{2,1,0:T(8,128)(2,1)}), s16[4,1008,256]{2,1,0:T(8,128)(2,1)S(1)}, u32[]{:S(2)}, u32[]{:S(2)}) async-start(s16[4,1008,256]{2,1,0:T(8,128)(2,1)} %partial_sums.3), calls=%async_computation.2 | async-start | bytes 4128768 | tf_op jit(solution)/shard_map/all_to_all | solution.py:256
  93.2 10.7 %collective-permute-start.5 = (bf16[1000,256]{1,0:T(8,128)(2,1)}, bf16[1000,256]{1,0:T(8,128)(2,1)S(1)}, u32[]{:S(2)}, u32[]{:S(2)}) collective-permute-start(bf16[1000,256]{1,0:T(8,128)(2,1)} %copy-done.2), channel_id=1, source_target_pairs={{0,1},{1,0},{2,3},{3,2},{4,5},{5,4},{6,7},{7,6},{8,9},{9,8},{10,11... | collective-permute-start | bytes 1536008 | tf_op jit(solution)/shard_map/ppermute | solution.py:252
  101.9 10.9 %collective-permute-start.6 = (bf16[1000,256]{1,0:T(8,128)(2,1)}, bf16[1000,256]{1,0:T(8,128)(2,1)S(1)}, u32[]{:S(2)}, u32[]{:S(2)}) collective-permute-start(bf16[1000,256]{1,0:T(8,128)(2,1)} %copy-done.2), channel_id=1, source_target_pairs={{0,31},{1,2},{2,1},{3,4},{4,3},{5,6},{6,5},{7,8},{8,7},{9,10},{10,... | collective-permute-start | bytes 1536008 | tf_op jit(solution)/shard_map/ppermute | solution.py:253
  112.8 1.0 copy-start.3
  115.5 1.0 copy-start.4
  116.5 1.2 %copy-start.5 = (f32[1000,256]{1,0:T(8,128)S(1)}, f32[1000,256]{1,0:T(8,128)}, u32[]{:S(2)}) copy-start(f32[1000,256]{1,0:T(8,128)} %copy-done.4) | copy-start | bytes 3072004
